TPU v7x, 32 devices: a whole 2x2x4 slice. The times are simulated.
32 devices in a mesh: group: 2 (over y), fsdp: 16 (over z, x, core).
Axes of the slice: x: 2, y: 2, z: 4, core: 2. Of those that a mesh axis runs over, the one named last changes fastest.
Arguments:
- acts: bfloat16 [2, 8192, 8192], P('group', 'fsdp'), may hold values from -6 to 6
- cotangent: bfloat16 [2, 8192, 512], P('group', 'fsdp'), may hold values from -5.40625 to 5.40625
- inner_params: float32 [2, 8192, 512], P('group', 'fsdp'), may hold values from -6 to 6
- adam_first: float32 [2, 8192, 512], P('group', 'fsdp'), may hold values from -0.018 to 0.018
- adam_second: float32 [2, 8192, 512], P('group', 'fsdp'), may hold values from 1e-06 to 0.0001
- inner_steps: int32 [2], replicated, may hold values from 8 to 128
- group_tokens: int32 [2], replicated, may hold values from 16384 to 131072
- anchor: float32 [8192, 512], P(('fsdp', 'group')), may hold values from -6 to 6
- momentum: float32 [8192, 512], P(('fsdp', 'group')), may hold values from -2 to 2
Outputs:
- new_anchor: float32 [8192, 512], P(('fsdp', 'group'))
- new_momentum: float32 [8192, 512], P(('fsdp', 'group'))
- group_weights: bfloat16 [2, 8192, 512], P('group', 'fsdp')
All inputs are finite; a program needn't handle non-finite values.
Results may differ from a plain program's by a relative error of at most 0.0004.
Values may be sent and summed in bfloat16 or wider, within the bound.
A program may use at most 128 MiB of HBM per device.

v0:
```python
import functools

import jax
import jax.numpy as jnp
import numpy as np
from jax import lax
from jax.experimental import pallas as pl
from jax.experimental.pallas import tpu as pltpu
from jax.sharding import PartitionSpec as P

beta_one = 0.9
beta_two = 0.95
epsilon = 1e-08
inner_rate = 0.3
decay_rate = 0.1
outer_rate = 0.7
outer_mom = 0.9


def inner_update(params, first_moment, second_moment, gradient, steps):
    fresh_first = beta_one * first_moment + (1.0 - beta_one) * gradient
    fresh_second = beta_two * second_moment + (1.0 - beta_two) * gradient * gradient
    steps_float = steps.astype(jnp.float32)
    correct_one = 1.0 - jnp.power(jnp.float32(beta_one), steps_float)
    correct_two = 1.0 - jnp.power(jnp.float32(beta_two), steps_float)
    ratio = fresh_first / correct_one / (jnp.sqrt(fresh_second / correct_two) + epsilon)
    return params - inner_rate * (ratio + decay_rate * params)


def outer_update(anchor, momentum, merged):
    pseudo = anchor - merged
    fresh_momentum = outer_mom * momentum + pseudo
    fresh_anchor = anchor - outer_rate * (pseudo + outer_mom * fresh_momentum)
    return (fresh_anchor, fresh_momentum)


def per_device(
    acts,
    cotangent,
    inner_params,
    adam_first,
    adam_second,
    inner_steps,
    group_tokens,
    anchor,
    momentum,
):
    fsdp_count = lax.axis_size("fsdp")
    group_index = lax.axis_index("group")
    inputs = acts[0]
    upstream = cotangent[0]
    group_total = inputs.shape[0] * fsdp_count
    contract = (((0,), (0,)), ((), ()))
    summed = lax.psum_scatter(
        lax.dot_general(inputs, upstream, contract, preferred_element_type=jnp.float32),
        "fsdp",
        scatter_dimension=0,
        tiled=True,
    )
    gradient = summed / group_total
    steps = lax.dynamic_index_in_dim(inner_steps, group_index, 0, False)
    updated = inner_update(inner_params[0], adam_first[0], adam_second[0], gradient, steps)
    counts = group_tokens.astype(jnp.float32)
    share = lax.dynamic_index_in_dim(counts, group_index, 0, False) / jnp.sum(counts)
    weighted = share * updated
    merged = lax.psum_scatter(weighted, "group", scatter_dimension=0, tiled=True)
    new_anchor, new_momentum = outer_update(anchor, momentum, merged)
    rebuilt = lax.all_gather(new_anchor.astype(jnp.bfloat16), "group", axis=0, tiled=True)
    return (new_anchor, new_momentum, rebuilt[None])


MESH = pl.DeviceIdType.MESH
WIRE = jnp.int16
LEVELS = 32767.0
SMALLEST = 1e-30
LINE = 4
FSDP = 16
GROUPS = 2
CORNER_PLAN = (
    ("pass", 1, 0, 0), ("pass", 1, 0, 1), ("cross", 0), ("start_x", 1, 0, 3), ("start_z", 1, 0),
    ("pass", 2, 0, 0), ("pass", 2, 0, 1), ("start_z", 1, 1), ("start_z", 1, 2),
    ("finish", 0, 0), ("finish", 0, 1),
    ("pass", 0, 1, 0), ("pass", 0, 1, 1), ("pass", 1, 1, 0), ("cross", 1), ("start_x", 1, 3, 4),
    ("pass", 1, 1, 1), ("pass", 2, 1, 0), ("pass", 2, 1, 1),
    ("finish", 1, 0), ("finish", 1, 1),
)
MIDDLE_PLAN = (
    ("pass_z", 2, 0), ("pass_z", 1, 0), ("pass", 0, 0, 0), ("pass", 0, 0, 1), ("cross", 0), ("start_x", 1, 0, 3),
    ("pass", 1, 0, 0), ("pass", 2, 0, 0), ("pass", 2, 0, 1), ("pass", 1, 0, 1),
    ("finish", 0, 0), ("pass_z", 0, 1), ("finish", 0, 1),
    ("pass_z", 2, 1), ("pass_z", 1, 1), ("cross", 1), ("start_x", 1, 3, 4),
    ("pass", 0, 1, 0), ("pass", 0, 1, 1), ("pass", 1, 1, 0), ("pass", 2, 1, 0), ("pass", 1, 1, 1), ("pass", 2, 1, 1),
    ("finish", 1, 0), ("finish", 1, 1),
)


def outer_step_kernel(
    group_total,
    steps_in,
    tokens_in,
    acts,
    cotangent,
    params_in,
    first_in,
    second_in,
    anchor_in,
    momentum_in,
    anchor_out,
    momentum_out,
    weights_out,
    steps_smem,
    tokens_smem,
    acts_buf,
    cot_buf,
    cot_t,
    own,
    far_z,
    x_send,
    x_recv,
    x_send_scale,
    x_recv_scale,
    z_send,
    z_send_scale,
    down_recv,
    down_scale,
    up_recv,
    up_scale,
    zz_send,
    zz_send_scale,
    down_z,
    down_z_scale,
    up_z,
    up_z_scale,
    cross_send,
    cross_recv,
    cross_send_scale,
    cross_recv_scale,
    params,
    first,
    second,
    anchor,
    momentum,
    weighted_send,
    weighted_recv,
    fresh_send,
    fresh_recv,
    local_sem,
    acts_send_sem,
    acts_recv_sem,
    cot_sem,
    state_sem,
    x_send_sem,
    x_recv_sem,
    z_send_sem,
    down_sem,
    up_sem,
    zz_send_sem,
    down_z_sem,
    up_z_sem,
    cross_sem,
    weighted_sem,
    fresh_sem,
):
    tokens, _ = acts.shape
    rows, width = params.shape
    half = rows // 2
    wide = width // 2
    line_width = width // 8
    cuts = ((0, wide), (wide, width - line_width))
    tail = slice(width - line_width, width)
    me = lax.axis_index("fsdp")
    group = lax.axis_index("group")
    other_group = 1 - group
    core, x, z = me % 2, (me // 2) % 2, me // 4
    lower = z < 2
    corner = (z == 0) | (z == LINE - 1)
    middle = jnp.logical_not(corner)
    toward = jnp.where(lower, 1, -1)

    sibling = (group, me + 1 - 2 * core)
    across = (group, me + 2 - 4 * x)
    above = (group, me + 4 * toward)
    below = (group, me - 4 * toward)
    peer = (other_group, me)

    def place(n):
        mid = jnp.where(n == 0, 3, jnp.where(n == 1, 0, jnp.where(n == 2, 2, 1)))
        level = jnp.where(corner, 3 - n, mid)
        return jnp.where(lower, level, 3 - level)

    def half_of(i):
        return (other_group + i) % 2

    def columns(n, far, i, owner_core):
        owner_x = jnp.where(far == 1, 1 - x, x)
        block = (place(n) * 2 + owner_x) * 2 + owner_core
        return pl.ds(pl.multiple_of(block * rows + half_of(i) * half, half), half)

    def acts_local(n, i, far):
        return pltpu.make_async_copy(
            acts.at[:, columns(n, far, i, core)],
            acts_buf.at[i, n, far, pl.ds(0, tokens)],
            local_sem.at[i, n, far],
        )

    def acts_remote(n, i, far):
        return pltpu.make_async_remote_copy(
            src_ref=acts.at[:, columns(n, far, i, 1 - core)],
            dst_ref=acts_buf.at[i, n, far, pl.ds(tokens, tokens)],
            send_sem=acts_send_sem.at[i, n, far],
            recv_sem=acts_recv_sem.at[i, n, far],
            device_id=sibling,
            device_id_type=MESH,
        )

    def remote(src, dst, send_sem, recv_sem, target):
        return pltpu.make_async_remote_copy(
            src_ref=src, dst_ref=dst, send_sem=send_sem, recv_sem=recv_sem, device_id=target, device_id_type=MESH
        )

    def x_copies(n, i, p):
        lo, hi = cuts[p]
        return (
            remote(
                x_send_scale.at[n, i, p], x_recv_scale.at[n, i, p],
                x_send_sem.at[n, i, p, 0], x_recv_sem.at[n, i, p, 0], across,
            ),
            remote(
                x_send.at[n, i, pl.ds(lo, hi - lo)], x_recv.at[n, i, pl.ds(lo, hi - lo)],
                x_send_sem.at[n, i, p, 1], x_recv_sem.at[n, i, p, 1], across,
            ),
        )

    def line_copies(n, i, p, into, scale, sem, slot, target):
        lo, hi = cuts[p]
        return (
            remote(
                z_send_scale.at[n, i, p], scale.at[slot, i, p],
                z_send_sem.at[n, i, p, 0], sem.at[slot, i, p, 0], target,
            ),
            remote(
                z_send.at[n, i, pl.ds(lo, hi - lo)], into.at[slot, i, pl.ds(lo, hi - lo)],
                z_send_sem.at[n, i, p, 1], sem.at[slot, i, p, 1], target,
            ),
        )

    def line_z_copies(n, i, into, scale, sem, slot, target):
        return (
            remote(
                zz_send_scale.at[n, i], scale.at[slot, i],
                zz_send_sem.at[n, i, 0], sem.at[slot, i, 0], target,
            ),
            remote(
                zz_send.at[n, i], into.at[slot, i],
                zz_send_sem.at[n, i, 1], sem.at[slot, i, 1], target,
            ),
        )

    def corner_send(n, i, p):
        return line_copies(n, i, p, down_recv, down_scale, down_sem, n, above)

    def middle_send(n, i, p):
        if n == 1:
            return line_copies(n, i, p, up_recv, up_scale, up_sem, 0, below)
        return line_copies(n, i, p, up_recv, up_scale, up_sem, n // 2, above)

    def corner_send_z(n, i):
        return line_z_copies(n, i, down_z, down_z_scale, down_z_sem, n, above)

    def middle_send_z(n, i):
        if n == 1:
            return line_z_copies(n, i, up_z, up_z_scale, up_z_sem, 0, below)
        return line_z_copies(n, i, up_z, up_z_scale, up_z_sem, n // 2, above)

    def from_below(slot, i, p):
        return line_copies(slot, i, p, down_recv, down_scale, down_sem, slot, below)

    def from_above(slot, i, p):
        return line_copies(slot, i, p, up_recv, up_scale, up_sem, slot, above)

    def cross_copies(i):
        return (
            remote(
                cross_send_scale.at[i], cross_recv_scale.at[i],
                cross_sem.at[0, i, 0], cross_sem.at[1, i, 0], across,
            ),
            remote(
                cross_send.at[i], cross_recv.at[i],
                cross_sem.at[0, i, 1], cross_sem.at[1, i, 1], across,
            ),
        )

    def weighted_copy(h):
        return remote(
            weighted_send.at[h], weighted_recv.at[h], weighted_sem.at[0, h], weighted_sem.at[1, h], peer
        )

    def fresh_copy(h):
        return remote(fresh_send.at[h], fresh_recv.at[h], fresh_sem.at[0, h], fresh_sem.at[1, h], peer)

    def start(copies):
        for copy in copies:
            copy.start()

    def arrived(copies):
        for copy in copies:
            copy.wait_recv()

    def left(copies):
        for copy in copies:
            copy.wait_send()

    state = []
    for n, (src, dst) in enumerate(
        (
            (params_in, params), (first_in, first), (second_in, second), (anchor_in, anchor), (momentum_in, momentum),
            (steps_in, steps_smem), (tokens_in, tokens_smem),
        )
    ):
        state.append(pltpu.make_async_copy(src, dst, state_sem.at[n]))
    cot_local = pltpu.make_async_copy(cotangent, cot_buf.at[pl.ds(0, tokens)], cot_sem.at[0])
    cot_remote = pltpu.make_async_remote_copy(
        src_ref=cotangent,
        dst_ref=cot_buf.at[pl.ds(tokens, tokens)],
        send_sem=cot_sem.at[1],
        recv_sem=cot_sem.at[2],
        device_id=sibling,
        device_id_type=MESH,
    )

    barrier = pltpu.get_barrier_semaphore()
    for target in (sibling, across, above, peer):
        pl.semaphore_signal(barrier, inc=1, device_id=target, device_id_type=MESH)

    @pl.when(middle)
    def _():
        pl.semaphore_signal(barrier, inc=1, device_id=below, device_id_type=MESH)

    order = [(n, i, far) for i in range(2) for n in range(LINE) for far in (1, 0)]
    cot_local.start()
    for n, i, far in order:
        acts_local(n, i, far).start()
    for copy in state:
        copy.start()
    pl.semaphore_wait(barrier, jnp.where(middle, 5, 4))
    cot_remote.start()
    for n, i, far in order:
        acts_remote(n, i, far).start()

    def encode(value):
        top = jnp.max(jnp.abs(value), axis=0, keepdims=True)
        levels = jnp.where(top > SMALLEST, LEVELS / jnp.maximum(top, SMALLEST), 0.0)
        return jnp.round(value * levels).astype(jnp.int32).astype(WIRE), top * (1.0 / LEVELS)

    def decode(coded, scale):
        return coded.astype(jnp.int32).astype(jnp.float32) * scale

    cot_local.wait()
    cot_t[:, 0:tokens] = cot_buf[0:tokens].astype(jnp.float32).T.astype(jnp.bfloat16)
    cot_remote.wait_recv()
    cot_t[:, tokens:] = cot_buf[tokens:].astype(jnp.float32).T.astype(jnp.bfloat16)

    def multiply(i):
        @pl.loop(0, LINE)
        def _(n):
            acts_local(n, i, 1).wait()
            acts_remote(n, i, 1).wait_recv()
            product = jnp.dot(cot_t[...], acts_buf[i, n, 1], preferred_element_type=jnp.float32)
            for p, (lo, hi) in enumerate(cuts):
                x_send[n, i, lo:hi], x_send_scale[n, i, p] = encode(product[lo:hi])
                if i == 0:
                    start(x_copies(n, i, p))
            far_z[n, i] = product[tail]
            acts_local(n, i, 0).wait()
            acts_remote(n, i, 0).wait_recv()
            own[n, i] = jnp.dot(cot_t[...], acts_buf[i, n, 0], preferred_element_type=jnp.float32)

            @pl.when(corner & (n < LINE - 1))
            def _():
                zz_send[n, i, 0], zz_send_scale[n, i, 0] = encode(own[n, i, tail])
                zz_send[n, i, 1], zz_send_scale[n, i, 1] = encode(far_z[n, i])
                if i == 0:
                    start(corner_send_z(n, i))

    def received(n, i, p):
        lo, hi = cuts[p]
        arrived(x_copies(n, i, p))
        return own[n, i, lo:hi] + decode(x_recv[n, i, lo:hi], x_recv_scale[n, i, p])

    def plus_line(total, n, i, p, into, scale, sem, slot, source):
        lo, hi = cuts[p]
        arrived(line_copies(0, i, p, into, scale, sem, slot, source))
        return total + decode(into[slot, i, lo:hi], scale[slot, i, p])

    def plus_below(total, i, p, slot):
        return plus_line(total, 0, i, p, down_recv, down_scale, down_sem, slot, below)

    def plus_above(total, i, p, slot):
        return plus_line(total, 0, i, p, up_recv, up_scale, up_sem, slot, above)

    def hand_on(role, n, i, p):
        lo, hi = cuts[p]
        total = received(n, i, p)
        if role == "middle":
            total = plus_above(total, i, p, 0) if n == 1 else plus_below(total, i, p, n // 2)
        z_send[n, i, lo:hi], z_send_scale[n, i, p] = encode(total)
        start(corner_send(n, i, p) if role == "corner" else middle_send(n, i, p))

    def line_z(i, above_slot, below_slot, n):
        if above_slot is not None:
            arrived(line_z_copies(0, i, up_z, up_z_scale, up_z_sem, above_slot, above))
        if below_slot is not None:
            arrived(line_z_copies(0, i, down_z, down_z_scale, down_z_sem, below_slot, below))
        totals = []
        for far in range(2):
            total = far_z[n, i] if far else own[n, i, tail]
            if above_slot is not None:
                total += decode(up_z[above_slot, i, far], up_z_scale[above_slot, i, far])
            if below_slot is not None:
                total += decode(down_z[below_slot, i, far], down_z_scale[below_slot, i, far])
            totals.append(total)
        return totals

    def hand_on_z(n, i):
        totals = line_z(i, 0, None, n) if n == 1 else line_z(i, None, n // 2, n)
        for far in range(2):
            zz_send[n, i, far], zz_send_scale[n, i, far] = encode(totals[far])
        start(middle_send_z(n, i))

    def cross_over(role, i):
        totals = line_z(i, 0, None, 3) if role == "corner" else line_z(i, 1, 2, 3)
        cross_send[i], cross_send_scale[i] = encode(totals[1])
        start(cross_copies(i))
        own[3, i, tail] = totals[0]

    def correction(beta):
        count = jnp.full((1, wide), steps_smem[group], jnp.int32).astype(jnp.float32)
        return 1.0 - jnp.exp(count * float(np.log(np.float64(np.float32(beta)))))

    def share_of(at):
        return jnp.full((1, wide), tokens_smem[at], jnp.int32).astype(jnp.float32)

    def finish(role, i, h):
        total = received(3, i, h)
        if role == "corner":
            total = plus_above(total, i, h, 0)
        else:
            total = plus_above(total, i, h, 1)
            total = plus_below(total, i, h, 2)
        if h == 1:
            arrived(cross_copies(i))
            total = jnp.concatenate([total, own[3, i, tail] + decode(cross_recv[i], cross_recv_scale[i])], axis=0)
        lanes = slice(h * wide, (h + 1) * wide)
        gradient = total.T / group_total
        at = pl.ds(pl.multiple_of(half_of(i) * half, half), half)
        weights = params[at, lanes]
        fresh_first = beta_one * first[at, lanes] + (1.0 - beta_one) * gradient
        fresh_second = beta_two * second[at, lanes] + (1.0 - beta_two) * gradient * gradient
        ratio = fresh_first / correction(beta_one) / (jnp.sqrt(fresh_second / correction(beta_two)) + epsilon)
        share = share_of(group) / (share_of(0) + share_of(1))
        weighted = share * (weights - inner_rate * (ratio + decay_rate * weights))
        if i == 0:
            weighted_send[h] = weighted
            weighted_copy(h).start()
            return
        weighted_copy(h).wait_recv()
        new_anchor, new_momentum = outer_update(anchor[:, lanes], momentum[:, lanes], weighted + weighted_recv[h])
        rounded = new_anchor.astype(jnp.bfloat16)
        fresh_send[h] = rounded
        fresh_copy(h).start()
        anchor_out[:, lanes] = new_anchor
        momentum_out[:, lanes] = new_momentum
        weights_out[at, lanes] = rounded

    def run(role, plan):
        for event in plan:
            kind, rest = event[0], event[1:]
            if kind == "pass":
                hand_on(role, *rest)
            elif kind == "pass_z":
                hand_on_z(*rest)
            elif kind == "cross":
                cross_over(role, *rest)
            elif kind == "start_x":
                for n in range(*rest[1:]):
                    for p in range(2):
                        start(x_copies(n, rest[0], p))
            elif kind == "start_z":
                start(corner_send_z(rest[1], rest[0]))
            else:
                finish(role, *rest)

    multiply(0)

    @pl.when(corner)
    def _():
        run("corner", (("pass", 0, 0, 0), ("pass", 0, 0, 1)))

    @pl.when(middle)
    def _():
        run("middle", (("pass_z", 0, 0),))

    for copy in state:
        copy.wait()
    multiply(1)

    @pl.when(corner)
    def _():
        run("corner", CORNER_PLAN)

    @pl.when(middle)
    def _():
        run("middle", MIDDLE_PLAN)

    theirs = pl.ds(pl.multiple_of(other_group * half, half), half)
    for h in range(2):
        fresh_copy(h).wait_recv()
        weights_out[theirs, h * wide : (h + 1) * wide] = fresh_recv[h]

    cot_remote.wait_send()
    for n, i, far in order:
        acts_remote(n, i, far).wait_send()
    for i in range(2):
        left(cross_copies(i))
        for n in range(LINE):
            for p in range(2):
                left(x_copies(n, i, p))
        for n in range(LINE - 1):
            left(line_z_copies(n, i, down_z, down_z_scale, down_z_sem, n, above))
            for p in range(2):
                left(corner_send(n, i, p))
    for h in range(2):
        weighted_copy(h).wait_send()
        fresh_copy(h).wait_send()


def write_out_kernel(anchor, momentum, weights, anchor_out, momentum_out, weights_out, sem):
    copies = [
        pltpu.make_async_copy(src, dst, sem.at[n])
        for n, (src, dst) in enumerate(((anchor, anchor_out), (momentum, momentum_out), (weights, weights_out)))
    ]
    for copy in copies:
        copy.start()
    for copy in copies:
        copy.wait()


def fused_per_device(
    acts, cotangent, inner_params, adam_first, adam_second, inner_steps, group_tokens, anchor, momentum
):
    tokens, _ = acts.shape[1:]
    rows, width = inner_params.shape[1:]
    half, wide, line_width = rows // 2, width // 2, width // 8
    low, full = jnp.bfloat16, jnp.float32
    dma = pltpu.SemaphoreType.DMA
    vmem = pltpu.VMEM
    body = width - line_width
    results = pl.pallas_call(
        functools.partial(outer_step_kernel, tokens * lax.axis_size("fsdp")),
        out_shape=(
            vmem(anchor.shape, full),
            vmem(anchor.shape, full),
            vmem((rows, width), low),
        ),
        in_specs=[pl.BlockSpec(memory_space=pl.ANY)] * 9,
        out_specs=[pl.BlockSpec(memory_space=pltpu.VMEM)] * 3,
        scratch_shapes=[
            pltpu.SMEM(inner_steps.shape, jnp.int32),
            pltpu.SMEM(group_tokens.shape, jnp.int32),
            vmem((2, LINE, 2, 2 * tokens, half), low),
            vmem((2 * tokens, width), low),
            vmem((width, 2 * tokens), low),
            vmem((LINE, 2, width, half), full),
            vmem((LINE, 2, line_width, half), full),
            vmem((LINE, 2, body, half), WIRE),
            vmem((LINE, 2, body, half), WIRE),
            vmem((LINE, 2, 2, 1, half), full),
            vmem((LINE, 2, 2, 1, half), full),
            vmem((3, 2, body, half), WIRE),
            vmem((3, 2, 2, 1, half), full),
            vmem((3, 2, body, half), WIRE),
            vmem((3, 2, 2, 1, half), full),
            vmem((2, 2, body, half), WIRE),
            vmem((2, 2, 2, 1, half), full),
            vmem((3, 2, 2, line_width, half), WIRE),
            vmem((3, 2, 2, 1, half), full),
            vmem((3, 2, 2, line_width, half), WIRE),
            vmem((3, 2, 2, 1, half), full),
            vmem((2, 2, 2, line_width, half), WIRE),
            vmem((2, 2, 2, 1, half), full),
            vmem((2, line_width, half), WIRE),
            vmem((2, line_width, half), WIRE),
            vmem((2, 1, half), full),
            vmem((2, 1, half), full),
            *[vmem((rows, width), full)] * 3,
            *[vmem((half, width), full)] * 2,
            *[vmem((2, half, wide), full)] * 2,
            *[vmem((2, half, wide), low)] * 2,
            *[dma((2, LINE, 2))] * 3,
            dma((3,)),
            dma((7,)),
            *[dma((LINE, 2, 2, 2))] * 2,
            dma((3, 2, 2, 2)),
            dma((3, 2, 2, 2)),
            dma((2, 2, 2, 2)),
            dma((3, 2, 2)),
            dma((3, 2, 2)),
            dma((2, 2, 2)),
            dma((2, 2, 2)),
            dma((2, 2)),
            dma((2, 2)),
        ],
        compiler_params=pltpu.CompilerParams(
            collective_id=0, has_side_effects=True, vmem_limit_bytes=48 * 1024 * 1024
        ),
    )(
        inner_steps, group_tokens, acts[0], cotangent[0], inner_params[0], adam_first[0], adam_second[0],
        anchor, momentum,
    )
    new_anchor, new_momentum, weights = pl.pallas_call(
        write_out_kernel,
        out_shape=(
            jax.ShapeDtypeStruct(anchor.shape, full),
            jax.ShapeDtypeStruct(anchor.shape, full),
            jax.ShapeDtypeStruct((rows, width), low),
        ),
        in_specs=[pl.BlockSpec(memory_space=pltpu.VMEM)] * 3,
        out_specs=[pl.BlockSpec(memory_space=pl.ANY)] * 3,
        scratch_shapes=[dma((3,))],
        compiler_params=pltpu.CompilerParams(vmem_limit_bytes=4 * 1024 * 1024),
    )(*results)
    return (new_anchor, new_momentum, weights[None])


def choose(*arguments):
    rows, width = arguments[2].shape[1:]
    fits = lax.axis_size("fsdp") == FSDP and lax.axis_size("group") == GROUPS
    if fits and rows % 256 == 0 and width % 256 == 0:
        return fused_per_device(*arguments)
    return per_device(*arguments)


def solution(mesh):
    placed = (
        P("group", "fsdp", None),
        P("group", "fsdp", None),
        P("group", "fsdp", None),
        P("group", "fsdp", None),
        P("group", "fsdp", None),
        P(),
        P(),
        P(("fsdp", "group"), None),
        P(("fsdp", "group"), None),
    )
    return jax.shard_map(
        choose,
        mesh=mesh,
        in_specs=placed,
        out_specs=(
            P(("fsdp", "group"), None),
            P(("fsdp", "group"), None),
            P("group", "fsdp", None),
        ),
        check_vma=False,
    )
```

profile of v0, /device:TPU:0, one launch (start us, length us, event | category | flops | bytes accessed | tf_op | source)
XLA Modules:
  0.0 67.2 jit_solution(13920719457824723118)
XLA Ops:
  0.6 0.0 copy-start
  0.6 1.2 %copy-done = f32[1,512,512]{2,1,0:T(8,128)S(1)} copy-done((f32[1,512,512]{2,1,0:T(8,128)S(1)}, f32[1,512,512]{2,1,0:T(8,128)}, u32[]{:S(2)}) %copy-start) | copy-done | bytes 1048600
  1.9 0.0 copy-start.1
  1.9 1.2 %copy-done.1 = f32[1,512,512]{2,1,0:T(8,128)S(1)} copy-done((f32[1,512,512]{2,1,0:T(8,128)S(1)}, f32[1,512,512]{2,1,0:T(8,128)}, u32[]{:S(2)}) %copy-start.1) | copy-done | bytes 1048600
  3.1 0.0 copy-start.2
  3.1 1.0 %copy-done.2 = bf16[1,512,512]{2,1,0:T(8,128)(2,1)S(1)} copy-done((bf16[1,512,512]{2,1,0:T(8,128)(2,1)S(1)}, bf16[1,512,512]{2,1,0:T(8,128)(2,1)}, u32[]{:S(2)}) %copy-start.2) | copy-done | bytes 524312
  4.1 0.0 copy-start.3
  4.1 1.0 %copy-done.3 = f32[256,512]{1,0:T(8,128)S(1)} copy-done((f32[256,512]{1,0:T(8,128)S(1)}, f32[256,512]{1,0:T(8,128)}, u32[]{:S(2)}) %copy-start.3) | copy-done | bytes 524312
  5.2 0.0 copy-start.4
  5.2 1.0 %copy-done.4 = f32[256,512]{1,0:T(8,128)S(1)} copy-done((f32[256,512]{1,0:T(8,128)S(1)}, f32[256,512]{1,0:T(8,128)}, u32[]{:S(2)}) %copy-start.4) | copy-done | bytes 524312
  6.2 0.0 copy-start.5
  6.2 0.7 copy-done.5
  6.9 0.0 copy-start.6
  6.9 0.7 copy-done.6
  7.5 58.5 %shard_map.112 = (f32[256,512]{1,0:T(8,128)S(1)}, f32[256,512]{1,0:T(8,128)S(1)}, bf16[512,512]{1,0:T(8,128)(2,1)S(1)}) custom-call(s32[2]{0:T(128)S(1)} %copy-done.5, s32[2]{0:T(128)S(1)} %copy-done.6, bf16[512,8192]{1,0:T(8,128)(2,1)} %bitcast.9, bf16[512,512]{1,0:T(8,128)(2,1)S(1)} %bitcast.8, f32[512,512]{1,0:T(8,128)S(1)} %bitcast.6, ...), custom_call_target="tpu_custom_call" | custom-call | tf_op jit(solution)/shard_map/pallas_call | solution.py:558
  66.0 1.2 %shard_map.113 = (f32[256,512]{1,0:T(8,128)}, f32[256,512]{1,0:T(8,128)}, bf16[512,512]{1,0:T(8,128)(2,1)}) custom-call(f32[256,512]{1,0:T(8,128)S(1)} %get-tuple-element.9.anchor, f32[256,512]{1,0:T(8,128)S(1)} %get-tuple-element.10.momentum, bf16[512,512]{1,0:T(8,128)(2,1)S(1)} %get-tuple-element.11.weights), custom_call_target="tpu_custom_call" | custom-call | tf_op jit(solution)/shard_map/pallas_call | solution.py:620
Async XLA Ops:
  0.6 1.2 %copy-start = (f32[1,512,512]{2,1,0:T(8,128)S(1)}, f32[1,512,512]{2,1,0:T(8,128)}, u32[]{:S(2)}) copy-start(f32[1,512,512]{2,1,0:T(8,128)} %param.11) | copy-start | bytes 3145732
  1.9 1.2 %copy-start.1 = (f32[1,512,512]{2,1,0:T(8,128)S(1)}, f32[1,512,512]{2,1,0:T(8,128)}, u32[]{:S(2)}) copy-start(f32[1,512,512]{2,1,0:T(8,128)} %param.12) | copy-start | bytes 3145732
  3.1 1.0 %copy-start.2 = (bf16[1,512,512]{2,1,0:T(8,128)(2,1)S(1)}, bf16[1,512,512]{2,1,0:T(8,128)(2,1)}, u32[]{:S(2)}) copy-start(bf16[1,512,512]{2,1,0:T(8,128)(2,1)} %param.10) | copy-start | bytes 1572868
  4.1 1.0 %copy-start.3 = (f32[256,512]{1,0:T(8,128)S(1)}, f32[256,512]{1,0:T(8,128)}, u32[]{:S(2)}) copy-start(f32[256,512]{1,0:T(8,128)} %anchor_in.1) | copy-start | bytes 1572868
  5.2 1.0 %copy-start.4 = (f32[256,512]{1,0:T(8,128)S(1)}, f32[256,512]{1,0:T(8,128)}, u32[]{:S(2)}) copy-start(f32[256,512]{1,0:T(8,128)} %momentum_in.1) | copy-start | bytes 1572868
  6.2 0.7 copy-start.5
  6.9 0.7 copy-start.6
where the time goes:
time: 67.5 us; the launch traced here: 67.2 us
  Pallas kernels  59.7 us (88%)
  local copies, waits for them, and re-layouts  6.87 us (10%)
    pallas_call x1, Pallas kernels, fused_per_device(): pl.pallas_call(functools.partial(outer_step_kernel, tokens * lax.axis_siz...  58.5 us
    unnamed x14, local copies, waits for them, and re-layouts  6.87 us

commit v1 on v0

--- a/solution.py
+++ b/solution.py
@@ -74,24 +74,28 @@
 LEVELS = 32767.0
 SMALLEST = 1e-30
 LINE = 4
+LINE_SHARE = 3
 FSDP = 16
 GROUPS = 2
 CORNER_PLAN = (
-    ("pass", 1, 0, 0), ("pass", 1, 0, 1), ("cross", 0), ("start_x", 1, 0, 3), ("start_z", 1, 0),
-    ("pass", 2, 0, 0), ("pass", 2, 0, 1), ("start_z", 1, 1), ("start_z", 1, 2),
-    ("finish", 0, 0), ("finish", 0, 1),
-    ("pass", 0, 1, 0), ("pass", 0, 1, 1), ("pass", 1, 1, 0), ("cross", 1), ("start_x", 1, 3, 4),
-    ("pass", 1, 1, 1), ("pass", 2, 1, 0), ("pass", 2, 1, 1),
+    ("pass", 1, 0, 0), ("pass", 1, 0, 1), ("cross", 0), ("start_x", 1, 0, 3),
+    ("pass", 2, 0, 0), ("pass", 2, 0, 1), ("finish", 0, 0), ("finish", 0, 1),
+    ("pass", 0, 1, 0), ("pass", 0, 1, 1), ("cross", 1), ("start_x", 1, 3, 4),
+    ("pass", 1, 1, 0), ("pass", 1, 1, 1), ("pass", 2, 1, 0), ("pass", 2, 1, 1),
     ("finish", 1, 0), ("finish", 1, 1),
 )
 MIDDLE_PLAN = (
-    ("pass_z", 2, 0), ("pass_z", 1, 0), ("pass", 0, 0, 0), ("pass", 0, 0, 1), ("cross", 0), ("start_x", 1, 0, 3),
-    ("pass", 1, 0, 0), ("pass", 2, 0, 0), ("pass", 2, 0, 1), ("pass", 1, 0, 1),
-    ("finish", 0, 0), ("pass_z", 0, 1), ("finish", 0, 1),
-    ("pass_z", 2, 1), ("pass_z", 1, 1), ("cross", 1), ("start_x", 1, 3, 4),
-    ("pass", 0, 1, 0), ("pass", 0, 1, 1), ("pass", 1, 1, 0), ("pass", 2, 1, 0), ("pass", 1, 1, 1), ("pass", 2, 1, 1),
+    ("pass_z", 2, 0), ("pass_z", 1, 0), ("pass", 0, 0, 0), ("pass", 0, 0, 1), ("pass_z", 0, 1),
+    ("cross", 0), ("start_x", 1, 0, 3), ("pass_z", 2, 1), ("pass", 1, 0, 0), ("pass", 2, 0, 0),
+    ("pass", 1, 0, 1), ("pass_z", 1, 1), ("pass", 2, 0, 1), ("cross", 1), ("start_x", 1, 3, 4),
+    ("finish", 0, 0), ("finish", 0, 1),
+    ("pass", 0, 1, 0), ("pass", 0, 1, 1), ("pass", 2, 1, 0), ("pass", 1, 1, 0), ("pass", 1, 1, 1), ("pass", 2, 1, 1),
     ("finish", 1, 0), ("finish", 1, 1),
 )
+
+
+def line_width_of(width):
+    return width * LINE_SHARE // 256 * 16
 
 
 def outer_step_kernel(
@@ -157,7 +161,8 @@
     zz_send_sem,
     down_z_sem,
     up_z_sem,
-    cross_sem,
+    cross_send_sem,
+    cross_recv_sem,
     weighted_sem,
     fresh_sem,
 ):
@@ -165,7 +170,7 @@
     rows, width = params.shape
     half = rows // 2
     wide = width // 2
-    line_width = width // 8
+    line_width = line_width_of(width)
     cuts = ((0, wide), (wide, width - line_width))
     tail = slice(width - line_width, width)
     me = lax.axis_index("fsdp")
@@ -207,7 +212,7 @@
         return pltpu.make_async_remote_copy(
             src_ref=acts.at[:, columns(n, far, i, 1 - core)],
             dst_ref=acts_buf.at[i, n, far, pl.ds(tokens, tokens)],
-            send_sem=acts_send_sem.at[i, n, far],
+            send_sem=acts_send_sem,
             recv_sem=acts_recv_sem.at[i, n, far],
             device_id=sibling,
             device_id_type=MESH,
@@ -223,11 +228,11 @@
         return (
             remote(
                 x_send_scale.at[n, i, p], x_recv_scale.at[n, i, p],
-                x_send_sem.at[n, i, p, 0], x_recv_sem.at[n, i, p, 0], across,
+                x_send_sem.at[0], x_recv_sem.at[n, i, p, 0], across,
             ),
             remote(
                 x_send.at[n, i, pl.ds(lo, hi - lo)], x_recv.at[n, i, pl.ds(lo, hi - lo)],
-                x_send_sem.at[n, i, p, 1], x_recv_sem.at[n, i, p, 1], across,
+                x_send_sem.at[1], x_recv_sem.at[n, i, p, 1], across,
             ),
         )
 
@@ -236,11 +241,11 @@
         return (
             remote(
                 z_send_scale.at[n, i, p], scale.at[slot, i, p],
-                z_send_sem.at[n, i, p, 0], sem.at[slot, i, p, 0], target,
+                z_send_sem.at[0], sem.at[slot, i, p, 0], target,
             ),
             remote(
                 z_send.at[n, i, pl.ds(lo, hi - lo)], into.at[slot, i, pl.ds(lo, hi - lo)],
-                z_send_sem.at[n, i, p, 1], sem.at[slot, i, p, 1], target,
+                z_send_sem.at[1], sem.at[slot, i, p, 1], target,
             ),
         )
 
@@ -248,11 +253,11 @@
         return (
             remote(
                 zz_send_scale.at[n, i], scale.at[slot, i],
-                zz_send_sem.at[n, i, 0], sem.at[slot, i, 0], target,
+                zz_send_sem.at[0], sem.at[slot, i, 0], target,
             ),
             remote(
                 zz_send.at[n, i], into.at[slot, i],
-                zz_send_sem.at[n, i, 1], sem.at[slot, i, 1], target,
+                zz_send_sem.at[1], sem.at[slot, i, 1], target,
             ),
         )
 
@@ -282,21 +287,21 @@
         return (
             remote(
                 cross_send_scale.at[i], cross_recv_scale.at[i],
-                cross_sem.at[0, i, 0], cross_sem.at[1, i, 0], across,
+                cross_send_sem.at[0], cross_recv_sem.at[i, 0], across,
             ),
             remote(
                 cross_send.at[i], cross_recv.at[i],
-                cross_sem.at[0, i, 1], cross_sem.at[1, i, 1], across,
+                cross_send_sem.at[1], cross_recv_sem.at[i, 1], across,
             ),
         )
 
     def weighted_copy(h):
         return remote(
-            weighted_send.at[h], weighted_recv.at[h], weighted_sem.at[0, h], weighted_sem.at[1, h], peer
+            weighted_send.at[h], weighted_recv.at[h], weighted_sem.at[2], weighted_sem.at[h], peer
         )
 
     def fresh_copy(h):
-        return remote(fresh_send.at[h], fresh_recv.at[h], fresh_sem.at[0, h], fresh_sem.at[1, h], peer)
+        return remote(fresh_send.at[h], fresh_recv.at[h], fresh_sem.at[2], fresh_sem.at[h], peer)
 
     def start(copies):
         for copy in copies:
@@ -305,10 +310,6 @@
     def arrived(copies):
         for copy in copies:
             copy.wait_recv()
-
-    def left(copies):
-        for copy in copies:
-            copy.wait_send()
 
     state = []
     for n, (src, dst) in enumerate(
@@ -379,8 +380,7 @@
             def _():
                 zz_send[n, i, 0], zz_send_scale[n, i, 0] = encode(own[n, i, tail])
                 zz_send[n, i, 1], zz_send_scale[n, i, 1] = encode(far_z[n, i])
-                if i == 0:
-                    start(corner_send_z(n, i))
+                start(corner_send_z(n, i))
 
     def received(n, i, p):
         lo, hi = cuts[p]
@@ -485,8 +485,6 @@
                 for n in range(*rest[1:]):
                     for p in range(2):
                         start(x_copies(n, rest[0], p))
-            elif kind == "start_z":
-                start(corner_send_z(rest[1], rest[0]))
             else:
                 finish(role, *rest)
 
@@ -518,20 +516,20 @@
         weights_out[theirs, h * wide : (h + 1) * wide] = fresh_recv[h]
 
     cot_remote.wait_send()
-    for n, i, far in order:
-        acts_remote(n, i, far).wait_send()
-    for i in range(2):
-        left(cross_copies(i))
-        for n in range(LINE):
-            for p in range(2):
-                left(x_copies(n, i, p))
-        for n in range(LINE - 1):
-            left(line_z_copies(n, i, down_z, down_z_scale, down_z_sem, n, above))
-            for p in range(2):
-                left(corner_send(n, i, p))
-    for h in range(2):
-        weighted_copy(h).wait_send()
-        fresh_copy(h).wait_send()
+    remote(acts_buf.at[0], acts_buf.at[0], acts_send_sem, acts_send_sem, sibling).wait_send()
+    for buffer, sem in (
+        (x_send_scale, x_send_sem.at[0]),
+        (x_send, x_send_sem.at[1]),
+        (z_send_scale, z_send_sem.at[0]),
+        (z_send, z_send_sem.at[1]),
+        (zz_send_scale, zz_send_sem.at[0]),
+        (zz_send, zz_send_sem.at[1]),
+        (cross_send_scale, cross_send_sem.at[0]),
+        (cross_send, cross_send_sem.at[1]),
+        (weighted_send, weighted_sem.at[2]),
+        (fresh_send, fresh_sem.at[2]),
+    ):
+        remote(buffer, buffer, sem, sem, sibling).wait_send()
 
 
 def write_out_kernel(anchor, momentum, weights, anchor_out, momentum_out, weights_out, sem):
@@ -550,11 +548,15 @@
 ):
     tokens, _ = acts.shape[1:]
     rows, width = inner_params.shape[1:]
-    half, wide, line_width = rows // 2, width // 2, width // 8
+    half, wide, line_width = rows // 2, width // 2, line_width_of(width)
     low, full = jnp.bfloat16, jnp.float32
     dma = pltpu.SemaphoreType.DMA
     vmem = pltpu.VMEM
     body = width - line_width
+    operands = (
+        inner_steps, group_tokens, acts[0], cotangent[0], inner_params[0], adam_first[0], adam_second[0],
+        anchor, momentum,
+    )
     results = pl.pallas_call(
         functools.partial(outer_step_kernel, tokens * lax.axis_size("fsdp")),
         out_shape=(
@@ -562,7 +564,7 @@
             vmem(anchor.shape, full),
             vmem((rows, width), low),
         ),
-        in_specs=[pl.BlockSpec(memory_space=pl.ANY)] * 9,
+        in_specs=[pl.BlockSpec(memory_space=pltpu.HBM)] * 9,
         out_specs=[pl.BlockSpec(memory_space=pltpu.VMEM)] * 3,
         scratch_shapes=[
             pltpu.SMEM(inner_steps.shape, jnp.int32),
@@ -596,27 +598,28 @@
             *[vmem((half, width), full)] * 2,
             *[vmem((2, half, wide), full)] * 2,
             *[vmem((2, half, wide), low)] * 2,
-            *[dma((2, LINE, 2))] * 3,
+            dma((2, LINE, 2)),
+            dma,
+            dma((2, LINE, 2)),
             dma((3,)),
             dma((7,)),
-            *[dma((LINE, 2, 2, 2))] * 2,
-            dma((3, 2, 2, 2)),
+            dma((2,)),
+            dma((LINE, 2, 2, 2)),
+            dma((2,)),
             dma((3, 2, 2, 2)),
             dma((2, 2, 2, 2)),
-            dma((3, 2, 2)),
+            dma((2,)),
             dma((3, 2, 2)),
             dma((2, 2, 2)),
-            dma((2, 2, 2)),
+            dma((2,)),
             dma((2, 2)),
-            dma((2, 2)),
+            dma((3,)),
+            dma((3,)),
         ],
         compiler_params=pltpu.CompilerParams(
             collective_id=0, has_side_effects=True, vmem_limit_bytes=48 * 1024 * 1024
         ),
-    )(
-        inner_steps, group_tokens, acts[0], cotangent[0], inner_params[0], adam_first[0], adam_second[0],
-        anchor, momentum,
-    )
+    )(*(pltpu.with_memory_space_constraint(operand, pltpu.HBM) for operand in operands))
     new_anchor, new_momentum, weights = pl.pallas_call(
         write_out_kernel,
         out_shape=(

time: 67.5 us -> 59 us (0.87)
  local copies, waits for them, and re-layouts: 6.87 us -> 0 us
  Pallas kernels: 59.7 us -> 58.2 us
    unnamed x14 -> x0, local copies, waits for them, and re-layouts: 6.87 us -> none
    pallas_call x1, Pallas kernels: 58.5 us -> 57 us  [fused_per_device(): pl.pallas_call(functools.partial(outer_step_kernel, tokens * lax.axis_siz...]
where the time goes in v1:
time: 59 us; the launch traced here: 58.8 us
  Pallas kernels  58.2 us (99%)
  between operations  0.64 us (1%)
    pallas_call x1, Pallas kernels, fused_per_device(): pl.pallas_call(functools.partial(outer_step_kernel, tokens * lax.axis_siz...  57 us

profile of v1, /device:TPU:0, one launch (start us, length us, event | category | flops | bytes accessed | tf_op | source)
XLA Modules:
  0.0 58.8 jit_solution(16119014790978336876)
XLA Ops:
  0.6 57.0 %shard_map.112 = (f32[256,512]{1,0:T(8,128)S(1)}, f32[256,512]{1,0:T(8,128)S(1)}, bf16[512,512]{1,0:T(8,128)(2,1)S(1)}) custom-call(s32[2]{0:T(128)} %steps_in.1, s32[2]{0:T(128)} %tokens_in.1, bf16[512,8192]{1,0:T(8,128)(2,1)} %bitcast.6, bf16[512,512]{1,0:T(8,128)(2,1)} %bitcast.10, f32[512,512]{1,0:T(8,128)} %bitcast.7, f32[512,512]{1,0:T(8,128)} %bitcast.8, ...), custom_call_target="tpu_custom_call" | custom-call | tf_op jit(solution)/shard_map/pallas_call | solution.py:560
  57.7 1.2 %shard_map.113 = (f32[256,512]{1,0:T(8,128)}, f32[256,512]{1,0:T(8,128)}, bf16[512,512]{1,0:T(8,128)(2,1)}) custom-call(f32[256,512]{1,0:T(8,128)S(1)} %get-tuple-element.9.anchor, f32[256,512]{1,0:T(8,128)S(1)} %get-tuple-element.10.momentum, bf16[512,512]{1,0:T(8,128)(2,1)S(1)} %get-tuple-element.11.weights), custom_call_target="tpu_custom_call" | custom-call | tf_op jit(solution)/shard_map/pallas_call | solution.py:623

commit v2 on v1

--- a/solution.py
+++ b/solution.py
@@ -74,28 +74,28 @@
 LEVELS = 32767.0
 SMALLEST = 1e-30
 LINE = 4
-LINE_SHARE = 3
 FSDP = 16
 GROUPS = 2
+MIDDLE_ROUTE = ((1, 0), (0, 1), (1, 2))
 CORNER_PLAN = (
-    ("pass", 1, 0, 0), ("pass", 1, 0, 1), ("cross", 0), ("start_x", 1, 0, 3),
-    ("pass", 2, 0, 0), ("pass", 2, 0, 1), ("finish", 0, 0), ("finish", 0, 1),
-    ("pass", 0, 1, 0), ("pass", 0, 1, 1), ("cross", 1), ("start_x", 1, 3, 4),
-    ("pass", 1, 1, 0), ("pass", 1, 1, 1), ("pass", 2, 1, 0), ("pass", 2, 1, 1),
-    ("finish", 1, 0), ("finish", 1, 1),
+    ("pass", 1, 0), ("cross", 0), ("start_x", 1, 0, 3), ("pass", 2, 0),
+    ("cross", 1), ("start_x", 1, 3, 4), ("pass", 0, 1), ("finish", 0), ("pass", 1, 1), ("pass", 2, 1), ("finish", 1),
 )
 MIDDLE_PLAN = (
-    ("pass_z", 2, 0), ("pass_z", 1, 0), ("pass", 0, 0, 0), ("pass", 0, 0, 1), ("pass_z", 0, 1),
-    ("cross", 0), ("start_x", 1, 0, 3), ("pass_z", 2, 1), ("pass", 1, 0, 0), ("pass", 2, 0, 0),
-    ("pass", 1, 0, 1), ("pass_z", 1, 1), ("pass", 2, 0, 1), ("cross", 1), ("start_x", 1, 3, 4),
-    ("finish", 0, 0), ("finish", 0, 1),
-    ("pass", 0, 1, 0), ("pass", 0, 1, 1), ("pass", 2, 1, 0), ("pass", 1, 1, 0), ("pass", 1, 1, 1), ("pass", 2, 1, 1),
-    ("finish", 1, 0), ("finish", 1, 1),
+    ("pass_z", 2, 0), ("pass", 0, 0), ("pass", 1, 0), ("cross", 0), ("start_x", 1, 0, 3), ("pass_z", 0, 1),
+    ("pass_z", 2, 1), ("pass", 2, 0), ("cross", 1), ("start_x", 1, 3, 4), ("finish", 0),
+    ("pass", 1, 1), ("pass", 0, 1), ("pass", 2, 1), ("finish", 1),
 )
 
 
 def line_width_of(width):
-    return width * LINE_SHARE // 256 * 16
+    return width // 16 * 6 // 32 * 16
+
+
+def cuts_of(width):
+    step, last = width // 4, width - line_width_of(width)
+    cuts = [(lo, min(lo + step, last)) for lo in range(0, last, step)]
+    return (cuts[-1], *cuts[:-1])
 
 
 def outer_step_kernel(
@@ -148,7 +148,8 @@
     weighted_recv,
     fresh_send,
     fresh_recv,
-    local_sem,
+    measure_buf,
+    vouch_sem,
     acts_send_sem,
     acts_recv_sem,
     cot_sem,
@@ -169,9 +170,9 @@
     tokens, _ = acts.shape
     rows, width = params.shape
     half = rows // 2
-    wide = width // 2
     line_width = line_width_of(width)
-    cuts = ((0, wide), (wide, width - line_width))
+    cuts = cuts_of(width)
+    parts = len(cuts)
     tail = slice(width - line_width, width)
     me = lax.axis_index("fsdp")
     group = lax.axis_index("group")
@@ -186,6 +187,7 @@
     across = (group, me + 2 - 4 * x)
     above = (group, me + 4 * toward)
     below = (group, me - 4 * toward)
+    beyond = (group, me + 8 * toward)
     peer = (other_group, me)
 
     def place(n):
@@ -205,7 +207,7 @@
         return pltpu.make_async_copy(
             acts.at[:, columns(n, far, i, core)],
             acts_buf.at[i, n, far, pl.ds(0, tokens)],
-            local_sem.at[i, n, far],
+            acts_recv_sem.at[i, n, far],
         )
 
     def acts_remote(n, i, far):
@@ -218,6 +220,15 @@
             device_id_type=MESH,
         )
 
+    def acts_arrived(n, i, far):
+        whole = acts_buf.at[i, n, far]
+        pltpu.make_async_copy(whole, whole, acts_recv_sem.at[i, n, far]).wait()
+
+    def fetch(n, i):
+        for far in (1, 0):
+            acts_local(n, i, far).start()
+            acts_remote(n, i, far).start()
+
     def remote(src, dst, send_sem, recv_sem, target):
         return pltpu.make_async_remote_copy(
             src_ref=src, dst_ref=dst, send_sem=send_sem, recv_sem=recv_sem, device_id=target, device_id_type=MESH
@@ -228,11 +239,11 @@
         return (
             remote(
                 x_send_scale.at[n, i, p], x_recv_scale.at[n, i, p],
-                x_send_sem.at[0], x_recv_sem.at[n, i, p, 0], across,
+                x_send_sem.at[0], x_recv_sem.at[n, i, p], across,
             ),
             remote(
                 x_send.at[n, i, pl.ds(lo, hi - lo)], x_recv.at[n, i, pl.ds(lo, hi - lo)],
-                x_send_sem.at[1], x_recv_sem.at[n, i, p, 1], across,
+                x_send_sem.at[1], x_recv_sem.at[n, i, p], across,
             ),
         )
 
@@ -241,11 +252,11 @@
         return (
             remote(
                 z_send_scale.at[n, i, p], scale.at[slot, i, p],
-                z_send_sem.at[0], sem.at[slot, i, p, 0], target,
+                z_send_sem.at[0], sem.at[slot, i, p], target,
             ),
             remote(
                 z_send.at[n, i, pl.ds(lo, hi - lo)], into.at[slot, i, pl.ds(lo, hi - lo)],
-                z_send_sem.at[1], sem.at[slot, i, p, 1], target,
+                z_send_sem.at[1], sem.at[slot, i, p], target,
             ),
         )
 
@@ -253,11 +264,11 @@
         return (
             remote(
                 zz_send_scale.at[n, i], scale.at[slot, i],
-                zz_send_sem.at[0], sem.at[slot, i, 0], target,
+                zz_send_sem.at[0], sem.at[slot, i], target,
             ),
             remote(
                 zz_send.at[n, i], into.at[slot, i],
-                zz_send_sem.at[1], sem.at[slot, i, 1], target,
+                zz_send_sem.at[1], sem.at[slot, i], target,
             ),
         )
 
@@ -265,51 +276,48 @@
         return line_copies(n, i, p, down_recv, down_scale, down_sem, n, above)
 
     def middle_send(n, i, p):
-        if n == 1:
-            return line_copies(n, i, p, up_recv, up_scale, up_sem, 0, below)
-        return line_copies(n, i, p, up_recv, up_scale, up_sem, n // 2, above)
+        slot, target = MIDDLE_ROUTE[n]
+        return line_copies(n, i, p, up_recv, up_scale, up_sem, slot, (beyond, below, above)[target])
 
     def corner_send_z(n, i):
         return line_z_copies(n, i, down_z, down_z_scale, down_z_sem, n, above)
 
     def middle_send_z(n, i):
-        if n == 1:
-            return line_z_copies(n, i, up_z, up_z_scale, up_z_sem, 0, below)
-        return line_z_copies(n, i, up_z, up_z_scale, up_z_sem, n // 2, above)
-
-    def from_below(slot, i, p):
-        return line_copies(slot, i, p, down_recv, down_scale, down_sem, slot, below)
-
-    def from_above(slot, i, p):
-        return line_copies(slot, i, p, up_recv, up_scale, up_sem, slot, above)
+        slot, target = MIDDLE_ROUTE[n]
+        return line_z_copies(n, i, up_z, up_z_scale, up_z_sem, slot, (beyond, below, above)[target])
 
     def cross_copies(i):
         return (
             remote(
                 cross_send_scale.at[i], cross_recv_scale.at[i],
-                cross_send_sem.at[0], cross_recv_sem.at[i, 0], across,
+                cross_send_sem.at[0], cross_recv_sem.at[i], across,
             ),
             remote(
                 cross_send.at[i], cross_recv.at[i],
-                cross_send_sem.at[1], cross_recv_sem.at[i, 1], across,
+                cross_send_sem.at[1], cross_recv_sem.at[i], across,
             ),
         )
 
+    def lanes_of(h):
+        return slice(cuts[h][0], cuts[h][1] if h > 0 else width)
+
     def weighted_copy(h):
+        at = lanes_of(h)
         return remote(
-            weighted_send.at[h], weighted_recv.at[h], weighted_sem.at[2], weighted_sem.at[h], peer
+            weighted_send.at[:, at], weighted_recv.at[:, at], weighted_sem.at[parts], weighted_sem.at[h], peer
         )
 
     def fresh_copy(h):
-        return remote(fresh_send.at[h], fresh_recv.at[h], fresh_sem.at[2], fresh_sem.at[h], peer)
+        at = lanes_of(h)
+        return remote(fresh_send.at[:, at], fresh_recv.at[:, at], fresh_sem.at[parts], fresh_sem.at[h], peer)
 
     def start(copies):
         for copy in copies:
             copy.start()
 
-    def arrived(copies):
-        for copy in copies:
-            copy.wait_recv()
+    def arrived(sem, coded_rows, scale_rows=1):
+        both = measure_buf.at[pl.ds(0, coded_rows // 2 + scale_rows)]
+        pltpu.make_async_copy(both, both, sem).wait()
 
     state = []
     for n, (src, dst) in enumerate(
@@ -337,16 +345,20 @@
     def _():
         pl.semaphore_signal(barrier, inc=1, device_id=below, device_id_type=MESH)
 
-    order = [(n, i, far) for i in range(2) for n in range(LINE) for far in (1, 0)]
     cot_local.start()
-    for n, i, far in order:
-        acts_local(n, i, far).start()
-    for copy in state:
-        copy.start()
+    for n in range(2):
+        for far in (1, 0):
+            acts_local(n, 0, far).start()
+    cot_local.wait()
+    cot_t[:, 0:tokens] = cot_buf[0:tokens].astype(jnp.float32).T.astype(jnp.bfloat16)
     pl.semaphore_wait(barrier, jnp.where(middle, 5, 4))
     cot_remote.start()
-    for n, i, far in order:
-        acts_remote(n, i, far).start()
+    for far in (1, 0):
+        acts_remote(0, 0, far).start()
+
+    @pl.when(middle)
+    def _():
+        pl.semaphore_signal(vouch_sem, inc=1, device_id=above, device_id_type=MESH)
 
     def encode(value):
         top = jnp.max(jnp.abs(value), axis=0, keepdims=True)
@@ -356,101 +368,114 @@
     def decode(coded, scale):
         return coded.astype(jnp.int32).astype(jnp.float32) * scale
 
-    cot_local.wait()
-    cot_t[:, 0:tokens] = cot_buf[0:tokens].astype(jnp.float32).T.astype(jnp.bfloat16)
     cot_remote.wait_recv()
+    for far in (1, 0):
+        acts_remote(1, 0, far).start()
+    for n in range(2, LINE):
+        fetch(n, 0)
     cot_t[:, tokens:] = cot_buf[tokens:].astype(jnp.float32).T.astype(jnp.bfloat16)
 
     def multiply(i):
         @pl.loop(0, LINE)
         def _(n):
-            acts_local(n, i, 1).wait()
-            acts_remote(n, i, 1).wait_recv()
-            product = jnp.dot(cot_t[...], acts_buf[i, n, 1], preferred_element_type=jnp.float32)
+            if i == 0:
+
+                @pl.when(n >= LINE // 2)
+                def _():
+                    fetch(2 * n - LINE, 1)
+                    fetch(2 * n - LINE + 1, 1)
+
+            acts_arrived(n, i, 1)
             for p, (lo, hi) in enumerate(cuts):
-                x_send[n, i, lo:hi], x_send_scale[n, i, p] = encode(product[lo:hi])
-                if i == 0:
+                product = jnp.dot(cot_t[lanes_of(p)], acts_buf[i, n, 1], preferred_element_type=jnp.float32)
+                x_send[n, i, lo:hi], x_send_scale[n, i, p] = encode(product[: hi - lo])
+                if p == 0:
+                    far_z[n, i] = product[hi - lo :]
+            if i == 0:
+                for p in range(parts):
                     start(x_copies(n, i, p))
-            far_z[n, i] = product[tail]
-            acts_local(n, i, 0).wait()
-            acts_remote(n, i, 0).wait_recv()
-            own[n, i] = jnp.dot(cot_t[...], acts_buf[i, n, 0], preferred_element_type=jnp.float32)
-
-            @pl.when(corner & (n < LINE - 1))
+            acts_arrived(n, i, 0)
+            for p in range(parts):
+                at = lanes_of(p)
+                own[n, i, at] = jnp.dot(cot_t[at], acts_buf[i, n, 0], preferred_element_type=jnp.float32)
+
+            @pl.when((corner & (n < LINE - 1)) | (middle & (n == 1)))
             def _():
                 zz_send[n, i, 0], zz_send_scale[n, i, 0] = encode(own[n, i, tail])
                 zz_send[n, i, 1], zz_send_scale[n, i, 1] = encode(far_z[n, i])
+
+            @pl.when(corner & (n < LINE - 1))
+            def _():
                 start(corner_send_z(n, i))
+
+            @pl.when(middle & (n == 1))
+            def _():
+                start(middle_send_z(1, i))
 
     def received(n, i, p):
         lo, hi = cuts[p]
-        arrived(x_copies(n, i, p))
+        arrived(x_recv_sem.at[n, i, p], hi - lo)
         return own[n, i, lo:hi] + decode(x_recv[n, i, lo:hi], x_recv_scale[n, i, p])
 
-    def plus_line(total, n, i, p, into, scale, sem, slot, source):
+    def plus_line(total, i, p, into, scale, sem, slot):
         lo, hi = cuts[p]
-        arrived(line_copies(0, i, p, into, scale, sem, slot, source))
+        arrived(sem.at[slot, i, p], hi - lo)
         return total + decode(into[slot, i, lo:hi], scale[slot, i, p])
 
     def plus_below(total, i, p, slot):
-        return plus_line(total, 0, i, p, down_recv, down_scale, down_sem, slot, below)
+        return plus_line(total, i, p, down_recv, down_scale, down_sem, slot)
 
     def plus_above(total, i, p, slot):
-        return plus_line(total, 0, i, p, up_recv, up_scale, up_sem, slot, above)
+        return plus_line(total, i, p, up_recv, up_scale, up_sem, slot)
 
     def hand_on(role, n, i, p):
         lo, hi = cuts[p]
         total = received(n, i, p)
-        if role == "middle":
-            total = plus_above(total, i, p, 0) if n == 1 else plus_below(total, i, p, n // 2)
+        if role == "middle" and n != 1:
+            total = plus_below(total, i, p, n // 2)
         z_send[n, i, lo:hi], z_send_scale[n, i, p] = encode(total)
         start(corner_send(n, i, p) if role == "corner" else middle_send(n, i, p))
 
-    def line_z(i, above_slot, below_slot, n):
-        if above_slot is not None:
-            arrived(line_z_copies(0, i, up_z, up_z_scale, up_z_sem, above_slot, above))
-        if below_slot is not None:
-            arrived(line_z_copies(0, i, down_z, down_z_scale, down_z_sem, below_slot, below))
-        totals = []
-        for far in range(2):
-            total = far_z[n, i] if far else own[n, i, tail]
-            if above_slot is not None:
-                total += decode(up_z[above_slot, i, far], up_z_scale[above_slot, i, far])
-            if below_slot is not None:
-                total += decode(down_z[below_slot, i, far], down_z_scale[below_slot, i, far])
-            totals.append(total)
+    def line_z(n, i, above_slots, below_slots):
+        streams = [(up_z, up_z_scale, up_z_sem, slot) for slot in above_slots]
+        streams += [(down_z, down_z_scale, down_z_sem, slot) for slot in below_slots]
+        totals = [own[n, i, tail], far_z[n, i]]
+        for into, scale, sem, slot in streams:
+            arrived(sem.at[slot, i], 2 * line_width, 2)
+            totals = [totals[far] + decode(into[slot, i, far], scale[slot, i, far]) for far in range(2)]
         return totals
 
     def hand_on_z(n, i):
-        totals = line_z(i, 0, None, n) if n == 1 else line_z(i, None, n // 2, n)
+        totals = line_z(n, i, (), (n // 2,))
         for far in range(2):
             zz_send[n, i, far], zz_send_scale[n, i, far] = encode(totals[far])
         start(middle_send_z(n, i))
 
     def cross_over(role, i):
-        totals = line_z(i, 0, None, 3) if role == "corner" else line_z(i, 1, 2, 3)
+        totals = line_z(3, i, (0, 1), ()) if role == "corner" else line_z(3, i, (1,), (2,))
         cross_send[i], cross_send_scale[i] = encode(totals[1])
         start(cross_copies(i))
         own[3, i, tail] = totals[0]
 
     def correction(beta):
-        count = jnp.full((1, wide), steps_smem[group], jnp.int32).astype(jnp.float32)
+        count = jnp.full((1, 1), steps_smem[group], jnp.int32).astype(jnp.float32)
         return 1.0 - jnp.exp(count * float(np.log(np.float64(np.float32(beta)))))
 
     def share_of(at):
-        return jnp.full((1, wide), tokens_smem[at], jnp.int32).astype(jnp.float32)
+        return jnp.full((1, 1), tokens_smem[at], jnp.int32).astype(jnp.float32)
 
     def finish(role, i, h):
         total = received(3, i, h)
         if role == "corner":
             total = plus_above(total, i, h, 0)
+            total = plus_above(total, i, h, 1)
         else:
             total = plus_above(total, i, h, 1)
             total = plus_below(total, i, h, 2)
-        if h == 1:
-            arrived(cross_copies(i))
+        if h == 0:
+            arrived(cross_recv_sem.at[i], line_width)
             total = jnp.concatenate([total, own[3, i, tail] + decode(cross_recv[i], cross_recv_scale[i])], axis=0)
-        lanes = slice(h * wide, (h + 1) * wide)
+        lanes = lanes_of(h)
         gradient = total.T / group_total
         at = pl.ds(pl.multiple_of(half_of(i) * half, half), half)
         weights = params[at, lanes]
@@ -460,13 +485,13 @@
         share = share_of(group) / (share_of(0) + share_of(1))
         weighted = share * (weights - inner_rate * (ratio + decay_rate * weights))
         if i == 0:
-            weighted_send[h] = weighted
+            weighted_send[:, lanes] = weighted
             weighted_copy(h).start()
             return
         weighted_copy(h).wait_recv()
-        new_anchor, new_momentum = outer_update(anchor[:, lanes], momentum[:, lanes], weighted + weighted_recv[h])
+        new_anchor, new_momentum = outer_update(anchor[:, lanes], momentum[:, lanes], weighted + weighted_recv[:, lanes])
         rounded = new_anchor.astype(jnp.bfloat16)
-        fresh_send[h] = rounded
+        fresh_send[:, lanes] = rounded
         fresh_copy(h).start()
         anchor_out[:, lanes] = new_anchor
         momentum_out[:, lanes] = new_momentum
@@ -476,31 +501,36 @@
         for event in plan:
             kind, rest = event[0], event[1:]
             if kind == "pass":
-                hand_on(role, *rest)
+                for p in range(parts):
+                    hand_on(role, *rest, p)
             elif kind == "pass_z":
                 hand_on_z(*rest)
             elif kind == "cross":
                 cross_over(role, *rest)
             elif kind == "start_x":
                 for n in range(*rest[1:]):
-                    for p in range(2):
+                    for p in range(parts):
                         start(x_copies(n, rest[0], p))
             else:
-                finish(role, *rest)
+                for h in range(parts):
+                    finish(role, *rest, h)
 
     multiply(0)
+    for copy in state:
+        copy.start()
 
     @pl.when(corner)
     def _():
-        run("corner", (("pass", 0, 0, 0), ("pass", 0, 0, 1)))
+        run("corner", (("pass", 0, 0),))
 
     @pl.when(middle)
     def _():
+        pl.semaphore_wait(vouch_sem, 1)
         run("middle", (("pass_z", 0, 0),))
 
+    multiply(1)
     for copy in state:
         copy.wait()
-    multiply(1)
 
     @pl.when(corner)
     def _():
@@ -511,9 +541,9 @@
         run("middle", MIDDLE_PLAN)
 
     theirs = pl.ds(pl.multiple_of(other_group * half, half), half)
-    for h in range(2):
+    for h in range(parts):
         fresh_copy(h).wait_recv()
-        weights_out[theirs, h * wide : (h + 1) * wide] = fresh_recv[h]
+        weights_out[theirs, lanes_of(h)] = fresh_recv[:, lanes_of(h)]
 
     cot_remote.wait_send()
     remote(acts_buf.at[0], acts_buf.at[0], acts_send_sem, acts_send_sem, sibling).wait_send()
@@ -526,8 +556,8 @@
         (zz_send, zz_send_sem.at[1]),
         (cross_send_scale, cross_send_sem.at[0]),
         (cross_send, cross_send_sem.at[1]),
-        (weighted_send, weighted_sem.at[2]),
-        (fresh_send, fresh_sem.at[2]),
+        (weighted_send, weighted_sem.at[parts]),
+        (fresh_send, fresh_sem.at[parts]),
     ):
         remote(buffer, buffer, sem, sem, sibling).wait_send()
 
@@ -548,11 +578,12 @@
 ):
     tokens, _ = acts.shape[1:]
     rows, width = inner_params.shape[1:]
-    half, wide, line_width = rows // 2, width // 2, line_width_of(width)
+    half, line_width = rows // 2, line_width_of(width)
     low, full = jnp.bfloat16, jnp.float32
     dma = pltpu.SemaphoreType.DMA
     vmem = pltpu.VMEM
     body = width - line_width
+    parts = len(cuts_of(width))
     operands = (
         inner_steps, group_tokens, acts[0], cotangent[0], inner_params[0], adam_first[0], adam_second[0],
         anchor, momentum,
@@ -576,14 +607,14 @@
             vmem((LINE, 2, line_width, half), full),
             vmem((LINE, 2, body, half), WIRE),
             vmem((LINE, 2, body, half), WIRE),
-            vmem((LINE, 2, 2, 1, half), full),
-            vmem((LINE, 2, 2, 1, half), full),
+            vmem((LINE, 2, parts, 1, half), full),
+            vmem((LINE, 2, parts, 1, half), full),
             vmem((3, 2, body, half), WIRE),
-            vmem((3, 2, 2, 1, half), full),
+            vmem((3, 2, parts, 1, half), full),
             vmem((3, 2, body, half), WIRE),
-            vmem((3, 2, 2, 1, half), full),
+            vmem((3, 2, parts, 1, half), full),
             vmem((2, 2, body, half), WIRE),
-            vmem((2, 2, 2, 1, half), full),
+            vmem((2, 2, parts, 1, half), full),
             vmem((3, 2, 2, line_width, half), WIRE),
             vmem((3, 2, 2, 1, half), full),
             vmem((3, 2, 2, line_width, half), WIRE),
@@ -596,25 +627,26 @@
             vmem((2, 1, half), full),
             *[vmem((rows, width), full)] * 3,
             *[vmem((half, width), full)] * 2,
-            *[vmem((2, half, wide), full)] * 2,
-            *[vmem((2, half, wide), low)] * 2,
-            dma((2, LINE, 2)),
+            *[vmem((half, width), full)] * 2,
+            *[vmem((half, width), low)] * 2,
+            vmem((max(width // 8, line_width) + 2, 1, half), full),
+            pltpu.SemaphoreType.REGULAR,
             dma,
             dma((2, LINE, 2)),
             dma((3,)),
             dma((7,)),
             dma((2,)),
-            dma((LINE, 2, 2, 2)),
+            dma((LINE, 2, parts)),
             dma((2,)),
-            dma((3, 2, 2, 2)),
-            dma((2, 2, 2, 2)),
+            dma((3, 2, parts)),
+            dma((2, 2, parts)),
             dma((2,)),
-            dma((3, 2, 2)),
-            dma((2, 2, 2)),
+            dma((3, 2)),
+            dma((2, 2)),
             dma((2,)),
-            dma((2, 2)),
-            dma((3,)),
-            dma((3,)),
+            dma((2,)),
+            dma((parts + 1,)),
+            dma((parts + 1,)),
         ],
         compiler_params=pltpu.CompilerParams(
             collective_id=0, has_side_effects=True, vmem_limit_bytes=48 * 1024 * 1024
@@ -638,7 +670,7 @@
 def choose(*arguments):
     rows, width = arguments[2].shape[1:]
     fits = lax.axis_size("fsdp") == FSDP and lax.axis_size("group") == GROUPS
-    if fits and rows % 256 == 0 and width % 256 == 0:
+    if fits and rows % 256 == 0 and width % 512 == 0:
         return fused_per_device(*arguments)
     return per_device(*arguments)
 

time: 59 us -> 55.7 us (0.944)
  Pallas kernels: 58.2 us -> 54.7 us
    pallas_call x1, Pallas kernels: 57 us -> 53.6 us  [fused_per_device(): pl.pallas_call(functools.partial(outer_step_kernel, tokens * lax.axis_siz...]
where the time goes in v2:
time: 55.7 us; the launch traced here: 55.4 us
  Pallas kernels  54.7 us (98%)
  between operations  0.64 us (1%)
    pallas_call x1, Pallas kernels, fused_per_device(): pl.pallas_call(functools.partial(outer_step_kernel, tokens * lax.axis_siz...  53.6 us
    pallas_call x1, Pallas kernels, fused_per_device(): pl.pallas_call(write_out_kernel, out_shape=(jax.ShapeDtypeStruct(anchor.s...  1.17 us

profile of v2, /device:TPU:0, one launch (start us, length us, event | category | flops | bytes accessed | tf_op | source)
XLA Modules:
  0.0 55.4 jit_solution(16422303352736170367)
XLA Ops:
  0.6 53.6 %shard_map.112 = (f32[256,512]{1,0:T(8,128)S(1)}, f32[256,512]{1,0:T(8,128)S(1)}, bf16[512,512]{1,0:T(8,128)(2,1)S(1)}) custom-call(s32[2]{0:T(128)} %steps_in.1, s32[2]{0:T(128)} %tokens_in.1, bf16[512,8192]{1,0:T(8,128)(2,1)} %bitcast.6, bf16[512,512]{1,0:T(8,128)(2,1)} %bitcast.10, f32[512,512]{1,0:T(8,128)} %bitcast.7, f32[512,512]{1,0:T(8,128)} %bitcast.8, ...), custom_call_target="tpu_custom_call" | custom-call | tf_op jit(solution)/shard_map/pallas_call | solution.py:591
  54.2 1.2 %shard_map.113 = (f32[256,512]{1,0:T(8,128)}, f32[256,512]{1,0:T(8,128)}, bf16[512,512]{1,0:T(8,128)(2,1)}) custom-call(f32[256,512]{1,0:T(8,128)S(1)} %get-tuple-element.9.anchor, f32[256,512]{1,0:T(8,128)S(1)} %get-tuple-element.10.momentum, bf16[512,512]{1,0:T(8,128)(2,1)S(1)} %get-tuple-element.11.weights), custom_call_target="tpu_custom_call" | custom-call | tf_op jit(solution)/shard_map/pallas_call | solution.py:655

commit v3 on v2

--- a/solution.py
+++ b/solution.py
@@ -349,12 +349,12 @@
     for n in range(2):
         for far in (1, 0):
             acts_local(n, 0, far).start()
-    cot_local.wait()
-    cot_t[:, 0:tokens] = cot_buf[0:tokens].astype(jnp.float32).T.astype(jnp.bfloat16)
     pl.semaphore_wait(barrier, jnp.where(middle, 5, 4))
     cot_remote.start()
     for far in (1, 0):
         acts_remote(0, 0, far).start()
+    for far in (1, 0):
+        acts_remote(1, 0, far).start()
 
     @pl.when(middle)
     def _():
@@ -368,9 +368,9 @@
     def decode(coded, scale):
         return coded.astype(jnp.int32).astype(jnp.float32) * scale
 
+    cot_local.wait()
+    cot_t[:, 0:tokens] = cot_buf[0:tokens].astype(jnp.float32).T.astype(jnp.bfloat16)
     cot_remote.wait_recv()
-    for far in (1, 0):
-        acts_remote(1, 0, far).start()
     for n in range(2, LINE):
         fetch(n, 0)
     cot_t[:, tokens:] = cot_buf[tokens:].astype(jnp.float32).T.astype(jnp.bfloat16)

time: 55.7 us -> 55.8 us (level)
  no operation moved by 1% of the time
where the time goes in v3:
time: 55.8 us; the launch traced here: 55.4 us
  Pallas kernels  54.7 us (98%)
  between operations  0.64 us (1%)
    pallas_call x1, Pallas kernels, fused_per_device(): pl.pallas_call(functools.partial(outer_step_kernel, tokens * lax.axis_siz...  53.6 us
    pallas_call x1, Pallas kernels, fused_per_device(): pl.pallas_call(write_out_kernel, out_shape=(jax.ShapeDtypeStruct(anchor.s...  1.17 us

profile of v3, /device:TPU:0, one launch (start us, length us, event | category | flops | bytes accessed | tf_op | source)
XLA Modules:
  0.0 55.4 jit_solution(17158805028356909675)
XLA Ops:
  0.6 53.6 %shard_map.112 = (f32[256,512]{1,0:T(8,128)S(1)}, f32[256,512]{1,0:T(8,128)S(1)}, bf16[512,512]{1,0:T(8,128)(2,1)S(1)}) custom-call(s32[2]{0:T(128)} %steps_in.1, s32[2]{0:T(128)} %tokens_in.1, bf16[512,8192]{1,0:T(8,128)(2,1)} %bitcast.6, bf16[512,512]{1,0:T(8,128)(2,1)} %bitcast.10, f32[512,512]{1,0:T(8,128)} %bitcast.7, f32[512,512]{1,0:T(8,128)} %bitcast.8, ...), custom_call_target="tpu_custom_call" | custom-call | tf_op jit(solution)/shard_map/pallas_call | solution.py:591
  54.2 1.2 %shard_map.113 = (f32[256,512]{1,0:T(8,128)}, f32[256,512]{1,0:T(8,128)}, bf16[512,512]{1,0:T(8,128)(2,1)}) custom-call(f32[256,512]{1,0:T(8,128)S(1)} %get-tuple-element.9.anchor, f32[256,512]{1,0:T(8,128)S(1)} %get-tuple-element.10.momentum, bf16[512,512]{1,0:T(8,128)(2,1)S(1)} %get-tuple-element.11.weights), custom_call_target="tpu_custom_call" | custom-call | tf_op jit(solution)/shard_map/pallas_call | solution.py:655

commit v4 on v3

--- a/solution.py
+++ b/solution.py
@@ -147,7 +147,6 @@
     weighted_send,
     weighted_recv,
     fresh_send,
-    fresh_recv,
     measure_buf,
     vouch_sem,
     acts_send_sem,
@@ -309,7 +308,8 @@
 
     def fresh_copy(h):
         at = lanes_of(h)
-        return remote(fresh_send.at[:, at], fresh_recv.at[:, at], fresh_sem.at[parts], fresh_sem.at[h], peer)
+        mine = pl.ds(pl.multiple_of(group * half, half), half)
+        return remote(fresh_send.at[:, at], weights_out.at[mine, at], fresh_sem.at[parts], fresh_sem.at[h], peer)
 
     def start(copies):
         for copy in copies:
@@ -540,10 +540,8 @@
     def _():
         run("middle", MIDDLE_PLAN)
 
-    theirs = pl.ds(pl.multiple_of(other_group * half, half), half)
     for h in range(parts):
         fresh_copy(h).wait_recv()
-        weights_out[theirs, lanes_of(h)] = fresh_recv[:, lanes_of(h)]
 
     cot_remote.wait_send()
     remote(acts_buf.at[0], acts_buf.at[0], acts_send_sem, acts_send_sem, sibling).wait_send()
@@ -628,7 +626,7 @@
             *[vmem((rows, width), full)] * 3,
             *[vmem((half, width), full)] * 2,
             *[vmem((half, width), full)] * 2,
-            *[vmem((half, width), low)] * 2,
+            vmem((half, width), low),
             vmem((max(width // 8, line_width) + 2, 1, half), full),
             pltpu.SemaphoreType.REGULAR,
             dma,

time: 55.8 us -> 55.8 us (level)
  no operation moved by 1% of the time
where the time goes in v4:
time: 55.8 us; the launch traced here: 55.4 us
  Pallas kernels  54.7 us (98%)
  between operations  0.64 us (1%)
    pallas_call x1, Pallas kernels, fused_per_device(): pl.pallas_call(functools.partial(outer_step_kernel, tokens * lax.axis_siz...  53.6 us
    pallas_call x1, Pallas kernels, fused_per_device(): pl.pallas_call(write_out_kernel, out_shape=(jax.ShapeDtypeStruct(anchor.s...  1.17 us

profile of v4, /device:TPU:0, one launch (start us, length us, event | category | flops | bytes accessed | tf_op | source)
XLA Modules:
  0.0 55.4 jit_solution(14808514116932577664)
XLA Ops:
  0.6 53.6 %shard_map.112 = (f32[256,512]{1,0:T(8,128)S(1)}, f32[256,512]{1,0:T(8,128)S(1)}, bf16[512,512]{1,0:T(8,128)(2,1)S(1)}) custom-call(s32[2]{0:T(128)} %steps_in.1, s32[2]{0:T(128)} %tokens_in.1, bf16[512,8192]{1,0:T(8,128)(2,1)} %bitcast.6, bf16[512,512]{1,0:T(8,128)(2,1)} %bitcast.10, f32[512,512]{1,0:T(8,128)} %bitcast.7, f32[512,512]{1,0:T(8,128)} %bitcast.8, ...), custom_call_target="tpu_custom_call" | custom-call | tf_op jit(solution)/shard_map/pallas_call | solution.py:589
  54.2 1.2 %shard_map.113 = (f32[256,512]{1,0:T(8,128)}, f32[256,512]{1,0:T(8,128)}, bf16[512,512]{1,0:T(8,128)(2,1)}) custom-call(f32[256,512]{1,0:T(8,128)S(1)} %get-tuple-element.9.anchor, f32[256,512]{1,0:T(8,128)S(1)} %get-tuple-element.10.momentum, bf16[512,512]{1,0:T(8,128)(2,1)S(1)} %get-tuple-element.11.weights), custom_call_target="tpu_custom_call" | custom-call | tf_op jit(solution)/shard_map/pallas_call | solution.py:653
